TPU v7x, 32 devices: a whole 2x2x4 slice. The times are simulated.
32 devices in a mesh: expert: 4 (over x, core), tensor: 8 (over z, y).
Axes of the slice: x: 2, y: 2, z: 4, core: 2. Of those that a mesh axis runs over, the one named last changes fastest.
Arguments:
- tokens: bfloat16 [128, 7168], P('expert', 'tensor'), may hold values from -6 to 6
- routes: int32 [128, 8], P('expert'), may hold values from 0 to 15, all different within a row; in each aligned block of 128 rows (0 to 127, 128 to 255, ...) at most 128 rows name the same one
- gates: bfloat16 [128, 8], P('expert'), may hold values from 0.099609375 to 0.59765625
- w_gate: bfloat16 [16, 2048, 7168], P('expert', 'tensor'), may hold values from -0.0625 to 0.0625
- w_up: bfloat16 [16, 2048, 7168], P('expert', 'tensor'), may hold values from -0.0625 to 0.0625
- w_down: bfloat16 [16, 2048, 7168], P('expert', None, 'tensor'), may hold values from -0.125 to 0.125
Outputs:
- moe_out: bfloat16 [128, 7168], P('expert', 'tensor')
Inputs may be any that keep to these rules, and one draw needn't show every extreme that they name: `routes`: each row names 8 different experts. No expert is named by more than 128 of the 128 rows, and one expert is named by exactly 128 rows.
All inputs are finite; a program needn't handle non-finite values.
Results may differ from a plain program's by a relative error of at most 0.0049.
Values may be sent and summed in bfloat16 or wider, within the bound.
A program may use at most 128 MiB of HBM per device.

v0:
```python
import jax
import jax.numpy as jnp
from jax import lax
from jax.sharding import PartitionSpec as P

CAP = 128


def entering(value, axis, combine, identity):
    length, index = (lax.axis_size(axis), lax.axis_index(axis))
    everything = lax.all_gather(value, axis)
    start = jnp.broadcast_to(jnp.asarray(identity, value.dtype), value.shape)

    def lap(k, before):
        reached = k < index
        new = combine(before, everything[k])
        return jnp.where(reached, new, before)

    return lax.fori_loop(0, length, lap, start)


def add_counts(earlier, later):
    return earlier + later


def on_device(tokens, routes, gates, w_gate, w_up, w_down):
    exp_dev = w_gate.shape[0]
    experts = exp_dev * lax.axis_size("expert")
    group_index = lax.axis_index("expert")
    expert_ids = jnp.arange(experts, dtype=jnp.int32)
    route_hits = routes[:, :, None] == expert_ids[None, None, :]
    member = jnp.sum(route_hits.astype(jnp.int32), axis=1)
    counts = jnp.sum(member, axis=0)
    offset = entering(counts, "expert", add_counts, jnp.zeros_like(counts))
    before = jnp.cumsum(member, axis=0) - member + offset[None, :]
    own_slot = jnp.sum(jnp.where(route_hits, before[:, None, :], 0), axis=2).astype(jnp.int32)
    all_routes, all_slots = (
        lax.all_gather(routes, "expert", axis=0, tiled=True),
        lax.all_gather(own_slot, "expert", axis=0, tiled=True),
    )
    row_block, all_gates = (
        lax.all_gather(tokens, "expert", axis=0, tiled=True),
        lax.all_gather(gates, "expert", axis=0, tiled=True),
    )
    gathered = lax.all_gather(row_block, "tensor", axis=1, tiled=True)
    local_ids = all_routes - group_index * exp_dev
    is_local = (local_ids >= 0) & (local_ids < exp_dev)
    slot_id = jnp.where(is_local, local_ids * CAP + all_slots, -1)
    slot_range = jnp.arange(exp_dev * CAP, dtype=jnp.int32)
    matches = slot_id[:, :, None] == slot_range[None, None, :]
    picked = jnp.any(matches, axis=1).astype(jnp.bfloat16)
    mixing = jnp.sum(jnp.where(matches, all_gates.astype(jnp.float32)[:, :, None], 0.0), axis=1)
    slot_rows = lax.dot_general(
        picked, gathered, (((0,), (0,)), ((), ())), preferred_element_type=jnp.float32
    ).astype(jnp.bfloat16)
    slot_rows = slot_rows.reshape(exp_dev, CAP, gathered.shape[1])
    gate_proj = jnp.einsum("ecd,efd->ecf", slot_rows, w_gate, preferred_element_type=jnp.float32)
    up_proj = jnp.einsum("ecd,efd->ecf", slot_rows, w_up, preferred_element_type=jnp.float32)
    hidden = (jax.nn.silu(gate_proj) * up_proj).astype(jnp.bfloat16)
    expert_out = jnp.einsum(
        "ecf,efd->ecd",
        lax.all_gather(hidden, "tensor", axis=2, tiled=True),
        w_down,
        preferred_element_type=jnp.float32,
    )
    expert_out = expert_out.reshape(exp_dev * CAP, w_down.shape[2])
    partial_value = jnp.dot(mixing, expert_out, precision=lax.Precision.HIGHEST)
    result = lax.psum_scatter(partial_value, "expert", scatter_dimension=0, tiled=True)
    return result.astype(jnp.bfloat16)


def solution(mesh):
    placed = (
        P("expert", "tensor"),
        P("expert", None),
        P("expert", None),
        P("expert", "tensor", None),
        P("expert", "tensor", None),
        P("expert", None, "tensor"),
    )
    return jax.shard_map(
        on_device, mesh=mesh, in_specs=placed, out_specs=P("expert", "tensor"), check_vma=False
    )
```

profile of v0, /device:TPU:0, one launch (start us, length us, event | category | flops | bytes accessed | tf_op | source)
XLA Modules:
  0.0 181.3 jit_solution(15544654380891682984)
XLA Ops:
  6.5 0.0 all-gather.7.cloned.1.call-start
  6.5 8.7 %all_gather.29 = bf16[128,896]{1,0:T(8,128)(2,1)} all-gather(bf16[32,896]{1,0:T(8,128)(2,1)} %param.8), channel_id=1, replica_groups=mesh['expert'=4,'tensor'=8] {'expert'}, dimensions={0}, use_global_device_ids=true | all-gather | bytes 286720 | tf_op jit(solution)/shard_map/all_gather | solution.py:42
  15.3 0.0 all-gather.7.cloned.1.call-update
  15.3 0.0 all-gather.9.cloned.1.call-start
  15.3 1.2 dynamic-slice
  17.2 0.8 convert_reduce_fusion
  18.0 0.2 dynamic-update-slice
  18.2 4.3 %all-reduce = s32[64]{0:T(128)S(1)} all-reduce(s32[64]{0:T(128)S(1)} %dynamic-update-slice), channel_id=2, replica_groups=mesh['expert'=4,'tensor'=8] {'expert'}, use_global_device_ids=true, to_apply=%add | all-reduce | flops 64 | bytes 512
  22.5 0.1 reshape.32
  22.6 0.1 copy.18
  22.6 0.1 reduce_window_sum.11
  22.7 0.1 while.14
  22.9 0.1 copy.20
  22.9 0.7 select_reduce_fusion.1
  23.7 5.2 %all-gather.2 = s32[4,32,8]{1,2,0:T(8,128)S(1)} all-gather(s32[1,32,8]{1,2,0:T(8,128)S(1)} %bitcast.29), channel_id=1, replica_groups=mesh['expert'=4,'tensor'=8] {'expert'}, dimensions={0}, use_global_device_ids=true | all-gather | bytes 5120 | tf_op jit(solution)/shard_map/all_gather | solution.py:39
  28.9 5.3 %all-gather.1 = s32[4,32,8]{1,2,0:T(8,128)S(1)} all-gather(s32[1,32,8]{1,2,0:T(8,128)} %bitcast.28), channel_id=1, replica_groups=mesh['expert'=4,'tensor'=8] {'expert'}, dimensions={0}, use_global_device_ids=true | all-gather | bytes 5120 | tf_op jit(solution)/shard_map/all_gather | solution.py:38
  34.2 0.1 copy.25
  34.3 0.7 fusion
  35.0 27.3 %all-gather.7.cloned.1.call-done = bf16[128,7168]{1,0:T(8,128)(2,1)} async-done(((bf16[128,896]{1,0:T(8,128)(2,1)}), bf16[128,7168]{1,0:T(8,128)(2,1)}) %all-gather.7.cloned.1.call-update) | async-done | bytes 1835024 | tf_op jit(solution)/shard_map/all_gather | solution.py:45
  62.3 6.6 %convolution_convert_fusion = bf16[512,7168]{1,0:T(8,128)(2,1)} fusion(pred[128,512]{1,0:T(8,128)(4,1)S(1)} %fusion, bf16[128,7168]{1,0:T(8,128)(2,1)} %all-gather.7.cloned.1.call-done), kind=kOutput, calls=%fused_computation.2 | convolution fusion | flops 943194112 | bytes 9240576 | tf_op jit(solution)/shard_map/dot_general | solution.py:53
  68.9 12.3 %fusion.2 = f32[4,128,256]{2,1,0:T(8,128)S(1)} fusion(bf16[4,128,7168]{2,1,0:T(8,128)(2,1)} %bitcast.22, bf16[4,256,7168]{2,1,0:T(8,128)(2,1)} %param.11), kind=kOutput, calls=%fused_computation.14 | convolution fusion | flops 1879048192 | bytes 22544384 | tf_op jit(solution)/shard_map/ecd,efd->ecf/dot_general | solution.py:57
  81.2 0.0 copy-start
  81.2 13.0 %fusion.1 = bf16[4,128,256]{2,1,0:T(8,128)(2,1)} fusion(bf16[4,128,7168]{2,1,0:T(8,128)(2,1)} %bitcast.23, bf16[4,256,7168]{2,1,0:T(8,128)(2,1)} %param.12, f32[4,128,256]{2,1,0:T(8,128)S(1)} %fusion.2), kind=kOutput, calls=%fused_computation.7 | convolution fusion | flops 1879834624 | bytes 22806528 | tf_op jit(solution)/shard_map/ecd,efd->ecf/dot_general | solution.py:58
  94.2 0.0 all-gather.9.cloned.1.call-update
  94.2 0.0 reduce-scatter.2.cloned.1.call-start
  94.3 0.0 copy-done
  94.3 5.4 %all-gather.3 = bf16[4,32,8]{1,2,0:T(8,128)(2,1)S(1)} all-gather(bf16[1,32,8]{1,2,0:T(8,128)(2,1)S(1)} %bitcast.30), channel_id=1, replica_groups=mesh['expert'=4,'tensor'=8] {'expert'}, dimensions={0}, use_global_device_ids=true | all-gather | bytes 2560 | tf_op jit(solution)/shard_map/all_gather | solution.py:43
  99.6 0.1 copy.26
  99.7 0.7 select_reduce_fusion
  100.4 43.1 %all-gather.9.cloned.1.call-done = bf16[4,128,2048]{2,1,0:T(8,128)(2,1)} async-done(((bf16[4,128,256]{2,1,0:T(8,128)(2,1)}), bf16[4,128,2048]{2,1,0:T(8,128)(2,1)}) %all-gather.9.cloned.1.call-update) | async-done | bytes 2097168 | tf_op jit(solution)/shard_map/all_gather | solution.py:62
  143.5 8.2 %fusion.3 = f32[4,128,896]{2,1,0:T(8,128)S(1)} fusion(bf16[4,128,2048]{2,1,0:T(8,128)(2,1)} %all-gather.9.cloned.1.call-done, bf16[4,2048,896]{2,1,0:T(8,128)(2,1)} %param.13), kind=kOutput, calls=%fused_computation.15 | convolution fusion | flops 1879048192 | bytes 18612224 | tf_op jit(solution)/shard_map/ecf,efd->ecd/dot_general | solution.py:60
  151.7 2.0 %fusion.4 = f32[128,896]{1,0:T(8,128)} fusion(f32[128,512]{1,0:T(8,128)S(1)} %select_reduce_fusion, f32[512,896]{1,0:T(8,128)S(1)} %bitcast.24), kind=kOutput, calls=%fused_computation.16 | convolution fusion | flops 704643072 | bytes 2555904 | tf_op jit(solution)/shard_map/dot_general | solution.py:67
  153.7 0.0 reduce-scatter.2.cloned.1.call-update
  153.7 19.5 %reduce-scatter.2.cloned.1.call-done = f32[32,896]{1,0:T(8,128)} async-done(((f32[128,896]{1,0:T(8,128)}), f32[32,896]{1,0:T(8,128)}) %reduce-scatter.2.cloned.1.call-update) | async-done | bytes 114704 | tf_op jit(solution)/shard_map/reduce_scatter | solution.py:68
  173.2 1.5 convert_element_type.20
  (8 shorter events, 0.1 us)
Async XLA Ops:
  6.5 55.8 %all-gather.7.cloned.1.call-start = ((), (), s32[]{:S(2)}) async-start(), calls=%async_computation.1 | async-start | bytes 2064384 | tf_op jit(solution)/shard_map/all_gather | solution.py:45
  15.3 128.3 %all-gather.9.cloned.1.call-start = ((), (), s32[]{:S(2)}) async-start(), calls=%async_computation.2 | async-start | bytes 2359296 | tf_op jit(solution)/shard_map/all_gather | solution.py:62
  81.2 13.1 %copy-start = (bf16[32,8]{0,1:T(8,128)(2,1)S(1)}, bf16[32,8]{0,1:T(8,128)(2,1)}, u32[]{:S(2)}) copy-start(bf16[32,8]{0,1:T(8,128)(2,1)} %param.10) | copy-start | bytes 1540
  94.2 79.0 %reduce-scatter.2.cloned.1.call-start = ((), (), s32[]{:S(2)}) async-start(), calls=%async_computation.3 | async-start | bytes 573440 | tf_op jit(solution)/shard_map/reduce_scatter | solution.py:68
Sparse Core Ops, SparseCore 0:
  15.4 46.8 all-gather.6
  94.3 49.1 all-gather.8
  153.8 19.3 reduce-scatter.1
where the time goes:
time: 182 us; the launch traced here: 181 us
  waiting for transfers between devices  90 us (49%)
  matrix products  42 us (23%)
  blocking collectives  28.9 us (16%)
  between operations  13.8 us (8%)
  other arithmetic  4.59 us (3%)
  local copies, waits for them, and re-layouts  1.88 us (1%)
    all_gather x1, waiting for transfers between devices, on_device(): lax.all_gather(hidden, 'tensor', axis=2, tiled=True)  43.1 us
    all_gather x1, waiting for transfers between devices, on_device(): gathered = lax.all_gather(row_block, 'tensor', axis=1, tiled=True)  27.3 us
    reduce_scatter x1, waiting for transfers between devices, on_device(): lax.psum_scatter(partial_value, 'expert', scatter_dimension=0, tiled=True)  19.5 us
    dot_general x1, matrix products, on_device(): jnp.einsum('ecd,efd->ecf', slot_rows, w_up, preferred_element_type=jnp.fl...  13 us
    dot_general x1, matrix products, on_device(): jnp.einsum('ecd,efd->ecf', slot_rows, w_gate, preferred_element_type=jnp....  12.3 us
    all_gather x1, blocking collectives, on_device(): lax.all_gather(tokens, 'expert', axis=0, tiled=True)  8.71 us
    dot_general x1, matrix products, on_device(): jnp.einsum('ecf,efd->ecd', lax.all_gather(hidden, 'tensor', axis=2, tiled...  8.16 us
    dot_general x1, matrix products, on_device(): lax.dot_general(picked, gathered, (((0,), (0,)), ((), ())), preferred_ele...  6.58 us
  transfers between devices with their start and end apart: 3, of which 3 were waited for; matrix products, arithmetic and copies ran while one was open for 3% of the time, Pallas kernels for 0%

commit v1 on v0

--- a/solution.py
+++ b/solution.py
@@ -42,7 +42,7 @@
         lax.all_gather(tokens, "expert", axis=0, tiled=True),
         lax.all_gather(gates, "expert", axis=0, tiled=True),
     )
-    gathered = lax.all_gather(row_block, "tensor", axis=1, tiled=True)
+    gathered = jnp.concatenate(lax.all_gather(row_block, "tensor"), 1)
     local_ids = all_routes - group_index * exp_dev
     is_local = (local_ids >= 0) & (local_ids < exp_dev)
     slot_id = jnp.where(is_local, local_ids * CAP + all_slots, -1)

time: 182 us -> 183 us (level)
  local copies, waits for them, and re-layouts: 1.88 us -> 5.12 us
    reshape x0 -> x1, local copies, waits for them, and re-layouts: none -> 3.16 us  [on_device(): gathered = jnp.concatenate(lax.all_gather(row_block, 'tensor'), 1)]
where the time goes in v1:
time: 183 us
  waiting for transfers between devices  89.5 us (49%)
  matrix products  40.5 us (22%)
  blocking collectives  28.9 us (16%)
  between operations  13.9 us (8%)
  local copies, waits for them, and re-layouts  5.12 us (3%)
  other arithmetic  4.59 us (3%)
    all_gather x1, waiting for transfers between devices, on_device(): lax.all_gather(hidden, 'tensor', axis=2, tiled=True)  43 us
    all_gather x1, waiting for transfers between devices, on_device(): gathered = jnp.concatenate(lax.all_gather(row_block, 'tensor'), 1)  27 us
    reduce_scatter x1, waiting for transfers between devices, on_device(): lax.psum_scatter(partial_value, 'expert', scatter_dimension=0, tiled=True)  19.5 us
    dot_general x1, matrix products, on_device(): jnp.einsum('ecd,efd->ecf', slot_rows, w_up, preferred_element_type=jnp.fl...  13 us
    dot_general x1, matrix products, on_device(): jnp.einsum('ecd,efd->ecf', slot_rows, w_gate, preferred_element_type=jnp....  12.3 us
    all_gather x1, blocking collectives, on_device(): lax.all_gather(tokens, 'expert', axis=0, tiled=True)  8.72 us
    dot_general x1, matrix products, on_device(): jnp.einsum('ecf,efd->ecd', lax.all_gather(hidden, 'tensor', axis=2, tiled...  8.16 us
    all_gather x1, blocking collectives, on_device(): lax.all_gather(gates, 'expert', axis=0, tiled=True)  5.37 us
  transfers between devices with their start and end apart: 3, of which 3 were waited for; matrix products, arithmetic and copies ran while one was open for 3% of the time, Pallas kernels for 0%

profile of v1, /device:TPU:0, one launch (start us, length us, event | category | flops | bytes accessed | tf_op | source)
XLA Modules:
  0.0 182.7 jit_solution(17152860726150036627)
XLA Ops:
  6.5 0.0 all-gather.10.cloned.1.call-start
  6.5 8.7 %all_gather.32 = bf16[128,896]{1,0:T(8,128)(2,1)} all-gather(bf16[32,896]{1,0:T(8,128)(2,1)} %param.8), channel_id=1, replica_groups=mesh['expert'=4,'tensor'=8] {'expert'}, dimensions={0}, use_global_device_ids=true | all-gather | bytes 286720 | tf_op jit(solution)/shard_map/all_gather | solution.py:42
  15.3 0.0 all-gather.10.cloned.1.call-update
  15.3 0.0 all-gather.8.cloned.1.call-start
  15.4 1.3 dynamic-slice
  17.4 0.8 convert_reduce_fusion
  18.2 0.2 dynamic-update-slice
  18.4 4.3 %all-reduce = s32[64]{0:T(128)S(1)} all-reduce(s32[64]{0:T(128)S(1)} %dynamic-update-slice), channel_id=2, replica_groups=mesh['expert'=4,'tensor'=8] {'expert'}, use_global_device_ids=true, to_apply=%add | all-reduce | flops 64 | bytes 512
  22.7 0.1 reshape.40
  22.8 0.1 copy.25
  22.8 0.1 reduce_window_sum.11
  22.9 0.1 while.14
  23.1 0.1 copy.27
  23.1 0.7 select_reduce_fusion.1
  23.9 5.2 %all-gather.3 = s32[4,32,8]{1,2,0:T(8,128)S(1)} all-gather(s32[1,32,8]{1,2,0:T(8,128)S(1)} %bitcast.34), channel_id=1, replica_groups=mesh['expert'=4,'tensor'=8] {'expert'}, dimensions={0}, use_global_device_ids=true | all-gather | bytes 5120 | tf_op jit(solution)/shard_map/all_gather | solution.py:39
  29.1 5.3 %all-gather.2 = s32[4,32,8]{1,2,0:T(8,128)S(1)} all-gather(s32[1,32,8]{1,2,0:T(8,128)} %bitcast.33), channel_id=1, replica_groups=mesh['expert'=4,'tensor'=8] {'expert'}, dimensions={0}, use_global_device_ids=true | all-gather | bytes 5120 | tf_op jit(solution)/shard_map/all_gather | solution.py:38
  34.4 0.1 copy.33
  34.5 0.7 fusion
  35.2 27.0 %all-gather.10.cloned.1.call-done = bf16[1024,896]{1,0:T(8,128)(2,1)} async-done(((bf16[128,896]{1,0:T(8,128)(2,1)}), bf16[1024,896]{1,0:T(8,128)(2,1)}) %all-gather.10.cloned.1.call-update) | async-done | bytes 1835024 | tf_op jit(solution)/shard_map/all_gather | solution.py:45
  62.2 3.2 %copy.32 = bf16[128,8,896]{0,2,1:T(8,128)(2,1)S(1)} copy(bf16[128,8,896]{2,0,1:T(8,128)(2,1)} %bitcast.29) | data formatting | bytes 3670016 | tf_op jit(solution)/shard_map/reshape | solution.py:45
  65.3 5.1 %convolution_convert_fusion = bf16[512,7168]{1,0:T(8,128)(2,1)} fusion(bf16[128,7168]{0,1:T(8,128)(2,1)S(1)} %bitcast.28, pred[128,512]{1,0:T(8,128)(4,1)S(1)} %fusion), kind=kOutput, calls=%fused_computation.2 | convolution fusion | flops 943259648 | bytes 9240576 | tf_op jit(solution)/shard_map/dot_general | solution.py:53
  70.4 12.3 %fusion.3 = f32[4,128,256]{2,1,0:T(8,128)S(1)} fusion(bf16[4,128,7168]{2,1,0:T(8,128)(2,1)} %bitcast.25, bf16[4,256,7168]{2,1,0:T(8,128)(2,1)} %param.11), kind=kOutput, calls=%fused_computation.15 | convolution fusion | flops 1879048192 | bytes 22544384 | tf_op jit(solution)/shard_map/ecd,efd->ecf/dot_general | solution.py:57
  82.7 0.0 copy-start
  82.7 13.0 %fusion.1 = bf16[4,128,256]{2,1,0:T(8,128)(2,1)} fusion(bf16[4,128,7168]{2,1,0:T(8,128)(2,1)} %bitcast.26, bf16[4,256,7168]{2,1,0:T(8,128)(2,1)} %param.12, f32[4,128,256]{2,1,0:T(8,128)S(1)} %fusion.3), kind=kOutput, calls=%fused_computation.7 | convolution fusion | flops 1879834624 | bytes 22806528 | tf_op jit(solution)/shard_map/ecd,efd->ecf/dot_general | solution.py:58
  95.7 0.0 all-gather.8.cloned.1.call-update
  95.7 0.0 reduce-scatter.2.cloned.1.call-start
  95.8 0.0 copy-done
  95.8 5.4 %all-gather.4 = bf16[4,32,8]{1,2,0:T(8,128)(2,1)S(1)} all-gather(bf16[1,32,8]{1,2,0:T(8,128)(2,1)S(1)} %bitcast.35), channel_id=1, replica_groups=mesh['expert'=4,'tensor'=8] {'expert'}, dimensions={0}, use_global_device_ids=true | all-gather | bytes 2560 | tf_op jit(solution)/shard_map/all_gather | solution.py:43
  101.1 0.1 copy.34
  101.2 0.7 select_reduce_fusion
  101.9 43.0 %all-gather.8.cloned.1.call-done = bf16[4,128,2048]{2,1,0:T(8,128)(2,1)} async-done(((bf16[4,128,256]{2,1,0:T(8,128)(2,1)}), bf16[4,128,2048]{2,1,0:T(8,128)(2,1)}) %all-gather.8.cloned.1.call-update) | async-done | bytes 2097168 | tf_op jit(solution)/shard_map/all_gather | solution.py:62
  144.9 8.2 %fusion.4 = f32[4,128,896]{2,1,0:T(8,128)S(1)} fusion(bf16[4,128,2048]{2,1,0:T(8,128)(2,1)} %all-gather.8.cloned.1.call-done, bf16[4,2048,896]{2,1,0:T(8,128)(2,1)} %param.13), kind=kOutput, calls=%fused_computation.16 | convolution fusion | flops 1879048192 | bytes 18612224 | tf_op jit(solution)/shard_map/ecf,efd->ecd/dot_general | solution.py:60
  153.1 2.0 %fusion.5 = f32[128,896]{1,0:T(8,128)} fusion(f32[128,512]{1,0:T(8,128)S(1)} %select_reduce_fusion, f32[512,896]{1,0:T(8,128)S(1)} %bitcast.27), kind=kOutput, calls=%fused_computation.17 | convolution fusion | flops 704643072 | bytes 2555904 | tf_op jit(solution)/shard_map/dot_general | solution.py:67
  155.1 0.0 reduce-scatter.2.cloned.1.call-update
  155.1 19.5 %reduce-scatter.2.cloned.1.call-done = f32[32,896]{1,0:T(8,128)} async-done(((f32[128,896]{1,0:T(8,128)}), f32[32,896]{1,0:T(8,128)}) %reduce-scatter.2.cloned.1.call-update) | async-done | bytes 114704 | tf_op jit(solution)/shard_map/reduce_scatter | solution.py:68
  174.6 1.5 convert_element_type.20
  (8 shorter events, 0.1 us)
Async XLA Ops:
  6.5 55.6 %all-gather.10.cloned.1.call-start = ((), (), s32[]{:S(2)}) async-start(), calls=%async_computation.3 | async-start | bytes 2064384 | tf_op jit(solution)/shard_map/all_gather | solution.py:45
  15.3 129.6 %all-gather.8.cloned.1.call-start = ((), (), s32[]{:S(2)}) async-start(), calls=%async_computation.1 | async-start | bytes 2359296 | tf_op jit(solution)/shard_map/all_gather | solution.py:62
  82.7 13.1 %copy-start = (bf16[32,8]{0,1:T(8,128)(2,1)S(1)}, bf16[32,8]{0,1:T(8,128)(2,1)}, u32[]{:S(2)}) copy-start(bf16[32,8]{0,1:T(8,128)(2,1)} %param.10) | copy-start | bytes 1540
  95.7 78.9 %reduce-scatter.2.cloned.1.call-start = ((), (), s32[]{:S(2)}) async-start(), calls=%async_computation.2 | async-start | bytes 573440 | tf_op jit(solution)/shard_map/reduce_scatter | solution.py:68
Sparse Core Ops, SparseCore 0:
  15.4 46.7 all-gather.9
  95.8 49.0 all-gather.7
  155.2 19.3 reduce-scatter.1
